TPU v7x, 32 devices: a whole 2x2x4 slice. The times are simulated.
32 devices in a mesh: dp: 4 (over y, core), expert: 4 (over z), tensor: 2 (over x).
Axes of the slice: x: 2, y: 2, z: 4, core: 2. Of those that a mesh axis runs over, the one named last changes fastest.
Arguments:
- router_input: bfloat16 [1024, 2048], P(('dp', 'expert'), 'tensor'), may hold values from -6 to 6
- router_weight: bfloat16 [2048, 8], replicated, may hold values from -0.125 to 0.125
- expert_ids: int32 [1024, 2], P(('dp', 'expert', 'tensor')), may hold values from 0 to 7, all different within a row; in each aligned block of 32 rows (0 to 31, 32 to 63, ...) at most 9 rows name the same one
- down_weight: bfloat16 [61440, 2048], P(('expert', 'tensor')), may hold values from -0.0625 to 0.0625
- hidden: bfloat16 [4, 72, 61440], P('dp', None, ('expert', 'tensor')), may hold values from -6 to 6
- grad_output: bfloat16 [1024, 2048], P(('dp', 'expert', 'tensor')), may hold values from -4 to 4
Outputs:
- weight_grad: bfloat16 [61440, 2048], P(('expert', 'tensor', 'dp'))
- hidden_grad: bfloat16 [4, 72, 61440], P('dp', None, ('expert', 'tensor'))
- router_grad: float32 [2048, 8], replicated
- input_grad: bfloat16 [1024, 2048], P(('dp', 'expert', 'tensor'))
Inputs may be any that keep to these rules, and one draw needn't show every extreme that they name: `expert_ids`: each row names 2 different experts. Within the 32 rows of one device no expert is named more than 9 times, and some device's rows name some expert exactly 9 times.
All inputs are finite; a program needn't handle non-finite values.
Results may differ from a plain program's by a relative error of at most 0.018.
Values may be sent and summed in bfloat16 or wider, within the bound.
A program may use at most 192 MiB of HBM per device.

v0:
```python
import jax
import jax.numpy as jnp
from jax import lax
from jax.sharding import PartitionSpec as P


def per_device(router_input, router_weight, expert_ids, down_weight, hidden, grad_output):
    token_rows = grad_output.shape[0]
    model_width = grad_output.shape[1]
    expert_count = router_weight.shape[1]
    choose_count = expert_ids.shape[1]
    expert_ranks = lax.axis_size("expert")
    tensor_ranks = lax.axis_size("tensor")
    sources = expert_ranks * tensor_ranks
    spread = sources // expert_count
    capacity = hidden.shape[1] // sources
    full_input = lax.all_to_all(router_input, "tensor", split_axis=0, concat_axis=1, tiled=True)
    logits = jnp.dot(full_input, router_weight, preferred_element_type=jnp.float32)
    labels = jnp.arange(expert_count, dtype=jnp.int32)
    onehot_int = (expert_ids[:, :, None] == labels).astype(jnp.int32)
    onehot = onehot_int.astype(jnp.float32)
    picked = jnp.sum(onehot * logits[:, None, :], axis=2)
    first_gate = jax.nn.sigmoid(picked[:, 0] - picked[:, 1])
    second_gate = jax.nn.sigmoid(picked[:, 1] - picked[:, 0])
    gate_values = jnp.stack([first_gate, second_gate], axis=1)
    gate_low = gate_values.astype(jnp.bfloat16)
    flat_hits = onehot_int.reshape(token_rows * choose_count, expert_count)
    before = jnp.cumsum(flat_hits, axis=0) - flat_hits
    slot_pos = jnp.sum(before * flat_hits, axis=1).reshape(token_rows, choose_count)
    slot_ids = jnp.arange(capacity, dtype=jnp.int32)
    dispatch_table = onehot[:, :, :, None] * (slot_pos[:, :, None, None] == slot_ids).astype(
        jnp.float32
    )
    slot_table = jnp.sum(dispatch_table, axis=1).astype(jnp.bfloat16)
    packed_grad = jnp.einsum(
        "rec,rd->ecd", slot_table, grad_output, preferred_element_type=jnp.float32
    ).astype(jnp.bfloat16)
    packed_gate = jnp.einsum("rkec,rk->ec", dispatch_table, gate_low.astype(jnp.float32)).astype(
        jnp.bfloat16
    )
    send_grad = jnp.repeat(packed_grad, spread, axis=0)
    send_gate = jnp.repeat(packed_gate, spread, axis=0)
    recv_grad, recv_gate = (
        lax.all_to_all(send_grad, ("expert", "tensor"), split_axis=0, concat_axis=0, tiled=True),
        lax.all_to_all(send_gate, ("expert", "tensor"), split_axis=0, concat_axis=0, tiled=True),
    )
    recv_grad = recv_grad.reshape(sources * capacity, model_width)
    recv_gate = recv_gate.reshape(sources * capacity).astype(jnp.float32)
    hidden_rows = hidden[0]
    gated_grad = (recv_gate[:, None] * recv_grad.astype(jnp.float32)).astype(jnp.bfloat16)
    expert_image = lax.dot_general(
        recv_grad, down_weight, (((1,), (1,)), ((), ())), preferred_element_type=jnp.float32
    )
    hidden_part = (recv_gate[:, None] * expert_image).astype(jnp.bfloat16)
    gate_partial = jnp.sum(hidden_rows.astype(jnp.float32) * expert_image, axis=1).reshape(
        sources, capacity
    )
    returned = lax.all_to_all(
        gate_partial, ("expert", "tensor"), split_axis=0, concat_axis=0, tiled=True
    )
    expert_sums = jnp.sum(returned.reshape(expert_count, spread, capacity), axis=1)
    gate_grad = jnp.einsum("rkec,ec->rk", dispatch_table, expert_sums)
    mixed_term = jnp.sum(gate_values * gate_grad, axis=1, keepdims=True)
    logit_part = gate_values * (gate_grad - mixed_term)
    logit_grad = jnp.sum(onehot * logit_part[:, :, None], axis=1)
    input_grad = jnp.dot(
        logit_grad, router_weight.astype(jnp.float32).T, precision=lax.Precision.HIGHEST
    ).astype(jnp.bfloat16)
    router_local = jnp.dot(
        full_input.astype(jnp.float32).T, logit_grad, precision=lax.Precision.HIGHEST
    )
    router_grad = lax.psum(router_local, ("dp", "expert", "tensor"))
    hidden_all = lax.all_to_all(hidden_rows, "dp", split_axis=1, concat_axis=0, tiled=True)
    gated_all = lax.all_gather(gated_grad, "dp", axis=0, tiled=True)
    weight_sum = lax.dot_general(
        hidden_all, gated_all, (((0,), (0,)), ((), ())), preferred_element_type=jnp.float32
    ).astype(jnp.bfloat16)
    return (weight_sum, hidden_part[None], router_grad, input_grad)


def solution(mesh):
    return jax.shard_map(
        per_device,
        mesh=mesh,
        in_specs=(
            P(("dp", "expert"), "tensor"),
            P(),
            P(("dp", "expert", "tensor"), None),
            P(("expert", "tensor"), None),
            P("dp", None, ("expert", "tensor")),
            P(("dp", "expert", "tensor"), None),
        ),
        out_specs=(
            P(("expert", "tensor", "dp"), None),
            P("dp", None, ("expert", "tensor")),
            P(),
            P(("dp", "expert", "tensor"), None),
        ),
        check_vma=False,
    )
```

profile of v0, /device:TPU:0, one launch (start us, length us, event | category | flops | bytes accessed | tf_op | source)
XLA Modules:
  0.0 210.3 jit_solution(2945085626296198110)
XLA Ops:
  8.0 0.0 copy-start
  8.0 4.4 %all-to-all-start = ((bf16[2,32,1024]{2,1,0:T(8,128)(2,1)}), bf16[2,32,1024]{2,1,0:T(8,128)(2,1)S(1)}, u32[]{:S(2)}, u32[]{:S(2)}) async-start(bf16[2,32,1024]{2,1,0:T(8,128)(2,1)} %bitcast.51), calls=%async_computation | async-start | bytes 262144 | tf_op jit(solution)/shard_map/all_to_all | solution.py:17
  12.4 0.8 copy.34
  13.1 0.7 convert_convert_fusion
  13.8 0.1 eq.49
  13.9 0.1 fusion.10
  14.0 0.1 reduce_window_sum.11
  14.1 0.2 select_reduce_fusion
  14.3 0.1 eq.53
  14.4 0.1 copy.35
  14.5 2.4 %all-to-all-done = bf16[2,32,1024]{2,1,0:T(8,128)(2,1)S(1)} async-done(((bf16[2,32,1024]{2,1,0:T(8,128)(2,1)}), bf16[2,32,1024]{2,1,0:T(8,128)(2,1)S(1)}, u32[]{:S(2)}, u32[]{:S(2)}) %all-to-all-start) | async-done | bytes 131104 | tf_op jit(solution)/shard_map/all_to_all | solution.py:17
  17.0 0.9 fusion.14
  17.9 0.7 multiply_reduce_fusion.2
  18.6 0.2 fusion.2
  18.8 0.1 copy.43
  18.9 0.6 copy.37
  19.5 5.4 %all-to-all-start.1 = ((bf16[8,1,9]{2,1,0:T(2,128)(2,1)}), bf16[8,1,9]{2,1,0:T(2,128)(2,1)S(1)}, u32[]{:S(2)}, u32[]{:S(2)}) async-start(bf16[8,1,9]{2,1,0:T(2,128)(2,1)} %copy.37), calls=%async_computation.1 | async-start | bytes 8192 | tf_op jit(solution)/shard_map/all_to_all | solution.py:45
  24.9 0.0 copy-done
  24.9 1.1 convolution_convert_fusion
  26.0 5.3 %all-to-all-done.1 = bf16[8,1,9]{2,1,0:T(2,128)(2,1)S(1)} async-done(((bf16[8,1,9]{2,1,0:T(2,128)(2,1)}), bf16[8,1,9]{2,1,0:T(2,128)(2,1)S(1)}, u32[]{:S(2)}, u32[]{:S(2)}) %all-to-all-start.1) | async-done | bytes 176 | tf_op jit(solution)/shard_map/all_to_all | solution.py:45
  31.3 3.5 %all-to-all-start.2 = ((bf16[8,9,2048]{2,1,0:T(8,128)(2,1)}), bf16[8,9,2048]{2,1,0:T(8,128)(2,1)S(1)}, u32[]{:S(2)}, u32[]{:S(2)}) async-start(bf16[8,9,2048]{2,1,0:T(8,128)(2,1)} %convolution_convert_fusion), calls=%async_computation.2 | async-start | bytes 1048576 | tf_op jit(solution)/shard_map/all_to_all | solution.py:44
  34.8 0.0 all-gather.2.cloned.1.call-start
  34.9 0.1 reshape.61
  35.0 12.0 %all-to-all-done.2 = bf16[8,9,2048]{2,1,0:T(8,128)(2,1)S(1)} async-done(((bf16[8,9,2048]{2,1,0:T(8,128)(2,1)}), bf16[8,9,2048]{2,1,0:T(8,128)(2,1)S(1)}, u32[]{:S(2)}, u32[]{:S(2)}) %all-to-all-start.2) | async-done | bytes 294944 | tf_op jit(solution)/shard_map/all_to_all | solution.py:44
  46.9 0.1 reshape.60
  47.1 0.8 multiply_convert_fusion.1
  47.9 0.0 all-gather.2.cloned.1.call-update
  47.9 0.0 copy-done.1
  47.9 15.6 %fusion = (f32[72]{0:T(128)S(1)}, bf16[1,72,7680]{2,1,0:T(8,128)(2,1)}) fusion(bf16[1,72,7680]{2,1,0:T(8,128)(2,1)S(1)} %copy-done.1, f32[72]{0:T(128)S(1)} %reshape.61, bf16[72,2048]{1,0:T(8,128)(2,1)S(1)} %reshape.60, bf16[7680,2048]{1,0:T(8,128)(2,1)} %param.9), kind=kOutput, calls=%fused_computation.5 | convolution fusion | flops 2267688960 | bytes 33964608 | tf_op jit(solution)/shard_map/dot_general | solution.py:51
  63.5 0.7 all_to_all.54
  64.2 3.8 %all-to-all-start.4 = ((f32[8,1,9]{2,1,0:T(1,128)}), f32[8,1,9]{2,1,0:T(1,128)S(1)}, u32[]{:S(2)}, u32[]{:S(2)}) async-start(f32[8,1,9]{2,1,0:T(1,128)} %bitcast.13), calls=%async_computation.4 | async-start | bytes 8192 | tf_op jit(solution)/shard_map/all_to_all | solution.py:58
  68.1 0.3 all_to_all.50
  68.4 1.1 copy.39
  69.5 5.0 %all-to-all-done.4 = f32[8,1,9]{2,1,0:T(1,128)S(1)} async-done(((f32[8,1,9]{2,1,0:T(1,128)}), f32[8,1,9]{2,1,0:T(1,128)S(1)}, u32[]{:S(2)}, u32[]{:S(2)}) %all-to-all-start.4) | async-done | bytes 320 | tf_op jit(solution)/shard_map/all_to_all | solution.py:58
  74.5 3.5 %all-to-all-start.3 = ((bf16[72,4,1920]{2,0,1:T(8,128)(2,1)}), bf16[72,4,1920]{2,0,1:T(8,128)(2,1)S(1)}, u32[]{:S(2)}, u32[]{:S(2)}) async-start(bf16[72,4,1920]{2,0,1:T(8,128)(2,1)} %copy.39), calls=%async_computation.3 | async-start | bytes 2211840 | tf_op jit(solution)/shard_map/all_to_all | solution.py:73
  78.0 0.0 all-reduce.2.cloned.1.call-start
  78.1 0.1 copy.49
  78.1 0.1 fusion.6
  78.3 0.0 copy-done.3
  78.3 0.8 convolution_bitcast_fusion
  79.1 0.0 all-reduce.2.cloned.1.call-update
  79.1 0.0 copy-done.2
  79.1 1.0 convolution_convert_fusion.1
  80.1 13.0 %all-to-all-done.3 = bf16[72,4,1920]{2,0,1:T(8,128)(2,1)S(1)} async-done(((bf16[72,4,1920]{2,0,1:T(8,128)(2,1)}), bf16[72,4,1920]{2,0,1:T(8,128)(2,1)S(1)}, u32[]{:S(2)}, u32[]{:S(2)}) %all-to-all-start.3) | async-done | bytes 1105952 | tf_op jit(solution)/shard_map/all_to_all | solution.py:73
  93.1 8.0 %convert_bitcast_fusion = bf16[1920,2048]{0,1:T(8,128)(2,1)} fusion(bf16[288,2048]{1,0:T(8,128)(2,1)} %all-gather.2.cloned.1.call-done, bf16[288,1920]{1,0:T(8,128)(2,1)S(1)} %bitcast.49), kind=kOutput, calls=%fused_computation | convolution fusion | flops 2268856320 | bytes 10149888 | tf_op jit(solution)/shard_map/dot_general | solution.py:75
  101.0 10.6 %copy.41 = bf16[1920,2048]{1,0:T(8,128)(2,1)} copy(bf16[1920,2048]{0,1:T(8,128)(2,1)} %convert_bitcast_fusion) | data formatting | bytes 15728640
  111.7 89.7 %all-reduce.2.cloned.1.call-done = f32[2048,8]{0,1:T(8,128)} async-done(((f32[2048,8]{0,1:T(8,128)}), f32[2048,8]{0,1:T(8,128)}) %all-reduce.2.cloned.1.call-update) | async-done | bytes 65552 | tf_op jit(solution)/shard_map/psum | solution.py:72
  201.4 1.5 copy.56
  (14 shorter events, 0.1 us)
Async XLA Ops:
  8.0 16.9 %copy-start = (bf16[32,2048]{1,0:T(8,128)(2,1)S(1)}, bf16[32,2048]{1,0:T(8,128)(2,1)}, u32[]{:S(2)}) copy-start(bf16[32,2048]{1,0:T(8,128)(2,1)} %param.11) | copy-start | bytes 393220
  8.0 8.9 %all-to-all-start = ((bf16[2,32,1024]{2,1,0:T(8,128)(2,1)}), bf16[2,32,1024]{2,1,0:T(8,128)(2,1)S(1)}, u32[]{:S(2)}, u32[]{:S(2)}) async-start(bf16[2,32,1024]{2,1,0:T(8,128)(2,1)} %bitcast.51), calls=%async_computation | async-start | bytes 262144 | tf_op jit(solution)/shard_map/all_to_all | solution.py:17
  19.5 11.8 %all-to-all-start.1 = ((bf16[8,1,9]{2,1,0:T(2,128)(2,1)}), bf16[8,1,9]{2,1,0:T(2,128)(2,1)S(1)}, u32[]{:S(2)}, u32[]{:S(2)}) async-start(bf16[8,1,9]{2,1,0:T(2,128)(2,1)} %copy.37), calls=%async_computation.1 | async-start | bytes 8192 | tf_op jit(solution)/shard_map/all_to_all | solution.py:45
  26.0 21.9 %copy-start.1 = (bf16[1,72,7680]{2,1,0:T(8,128)(2,1)S(1)}, bf16[1,72,7680]{2,1,0:T(8,128)(2,1)}, u32[]{:S(2)}) copy-start(bf16[1,72,7680]{2,1,0:T(8,128)(2,1)} %param.10) | copy-start | bytes 3317764
  31.3 15.6 %all-to-all-start.2 = ((bf16[8,9,2048]{2,1,0:T(8,128)(2,1)}), bf16[8,9,2048]{2,1,0:T(8,128)(2,1)S(1)}, u32[]{:S(2)}, u32[]{:S(2)}) async-start(bf16[8,9,2048]{2,1,0:T(8,128)(2,1)} %convolution_convert_fusion), calls=%async_computation.2 | async-start | bytes 1048576 | tf_op jit(solution)/shard_map/all_to_all | solution.py:44
  34.8 58.2 %all-gather.2.cloned.1.call-start = ((), (), s32[]{:S(2)}) async-start(), calls=%async_computation.5 | async-start | bytes 1474560 | tf_op jit(solution)/shard_map/all_gather | solution.py:74
  64.2 10.3 %all-to-all-start.4 = ((f32[8,1,9]{2,1,0:T(1,128)}), f32[8,1,9]{2,1,0:T(1,128)S(1)}, u32[]{:S(2)}, u32[]{:S(2)}) async-start(f32[8,1,9]{2,1,0:T(1,128)} %bitcast.13), calls=%async_computation.4 | async-start | bytes 8192 | tf_op jit(solution)/shard_map/all_to_all | solution.py:58
  69.5 8.8 %copy-start.3 = (s32[32,2]{0,1:T(2,128)S(1)}, s32[32,2]{0,1:T(2,128)}, u32[]{:S(2)}) copy-start(s32[32,2]{0,1:T(2,128)} %param.8) | copy-start | bytes 772
  69.5 9.6 %copy-start.2 = (bf16[2048,8]{0,1:T(8,128)(2,1)S(1)}, bf16[2048,8]{0,1:T(8,128)(2,1)}, u32[]{:S(2)}) copy-start(bf16[2048,8]{0,1:T(8,128)(2,1)} %param.7) | copy-start | bytes 98308
  74.5 18.6 %all-to-all-start.3 = ((bf16[72,4,1920]{2,0,1:T(8,128)(2,1)}), bf16[72,4,1920]{2,0,1:T(8,128)(2,1)S(1)}, u32[]{:S(2)}, u32[]{:S(2)}) async-start(bf16[72,4,1920]{2,0,1:T(8,128)(2,1)} %copy.39), calls=%async_computation.3 | async-start | bytes 2211840 | tf_op jit(solution)/shard_map/all_to_all | solution.py:73
  78.0 123.4 %all-reduce.2.cloned.1.call-start = ((), (), s32[]{:S(2)}) async-start(), calls=%async_computation.6 | async-start | bytes 131072 | tf_op jit(solution)/shard_map/psum | solution.py:72
Sparse Core Ops, SparseCore 0:
  48.0 16.5 all-gather.1
Sparse Core Ops, SparseCore 1:
  84.7 116.6 all-reduce.1
where the time goes:
time: 212 us; the launch traced here: 210 us
  waiting for transfers between devices  127 us (60%)
  matrix products  27.5 us (13%)
  starting transfers between devices  20.7 us (10%)
  local copies, waits for them, and re-layouts  16.3 us (8%)
  between operations  15.6 us (7%)
  other arithmetic  2.78 us (1%)
    psum x1, waiting for transfers between devices, per_device(): router_grad = lax.psum(router_local, ('dp', 'expert', 'tensor'))  89.7 us
    dot_general x1, matrix products, per_device(): lax.dot_general(recv_grad, down_weight, (((1,), (1,)), ((), ())), preferr...  15.6 us
    all_to_all x1, waiting for transfers between devices, per_device(): lax.all_to_all(hidden_rows, 'dp', split_axis=1, concat_axis=0, tiled=True)  13 us
    unnamed x12, local copies, waits for them, and re-layouts  13 us
    all_to_all x1, waiting for transfers between devices, per_device(): lax.all_to_all(send_grad, ('expert', 'tensor'), split_axis=0, concat_axis...  12 us
    dot_general x1, matrix products, per_device(): lax.dot_general(hidden_all, gated_all, (((0,), (0,)), ((), ())), preferre...  7.96 us
    all_to_all x1, starting transfers between devices, per_device(): lax.all_to_all(send_gate, ('expert', 'tensor'), split_axis=0, concat_axis...  5.41 us
    all_to_all x1, waiting for transfers between devices, per_device(): lax.all_to_all(send_gate, ('expert', 'tensor'), split_axis=0, concat_axis...  5.34 us
  transfers between devices with their start and end apart: 7, of which 6 were waited for; matrix products, arithmetic and copies ran while one was open for 19% of the time, Pallas kernels for 0%

commit v1 on v0

--- a/solution.py
+++ b/solution.py
@@ -1,10 +1,468 @@
+import functools
+
 import jax
 import jax.numpy as jnp
 from jax import lax
+from jax.experimental import pallas as pl
+from jax.experimental.pallas import tpu as pltpu
 from jax.sharding import PartitionSpec as P
 
 
-def per_device(router_input, router_weight, expert_ids, down_weight, hidden, grad_output):
+PAD = 16
+LANES = 128
+VMEM_LIMIT = 64 * 1000 * 1000
+EXACT = lax.Precision.HIGHEST
+CONTRACT_LAST = (((1,), (1,)), ((), ()))
+CONTRACT_FIRST = (((0,), (0,)), ((), ()))
+
+
+def iota(shape, axis):
+    return lax.broadcasted_iota(jnp.int32, shape, axis)
+
+
+def exchange_kernel(
+    groups, expert_ranks, tensor_ranks, capacity, tile,
+    ids_ref, router_weight_ref, grad_ref, router_input_ref, down_ref, hidden_ref,
+    hidden_grad_ref, input_grad_ref, router_grad_ref, hidden_all_ref, gated_all_ref,
+    weights, hidden_rows, full_input, send_grad, recv_grad, send_gate, recv_gate,
+    send_back, recv_back, send_sum, recv_sum, packed, gate_acc,
+    weight_sem, hidden_sem, own_sem,
+    input_send, input_recv, hidden_send, hidden_recv, grad_send, grad_recv,
+    gate_send, gate_recv, gated_send, gated_recv, back_send, back_recv,
+    sum_send, sum_recv, whole_send, whole_recv,
+):
+    f32, bf16 = jnp.float32, jnp.bfloat16
+    group = lax.axis_index("dp")
+    tensor = lax.axis_index("tensor")
+    sources = expert_ranks * tensor_ranks
+    source = lax.axis_index("expert") * tensor_ranks + tensor
+    devices = groups * sources
+    me = group * sources + source
+    slots, width = hidden_ref.shape
+    part = width // groups
+    experts = router_weight_ref.shape[0]
+    tokens = grad_ref.shape[0]
+    span = router_input_ref.shape[1]
+    rows = sources * PAD
+    tiles = width // tile
+
+    def place(d, x):
+        return {"dp": d, "expert": x // tensor_ranks, "tensor": x % tensor_ranks}
+
+    def remote(src, dst, send, recv, device):
+        return pltpu.make_async_remote_copy(
+            src_ref=src, dst_ref=dst, send_sem=send, recv_sem=recv,
+            device_id=device, device_id_type=pl.DeviceIdType.MESH,
+        )
+
+    def weight_copy(i):
+        return pltpu.make_async_copy(
+            down_ref.at[pl.ds(i * tile, tile)], weights.at[i], weight_sem.at[i]
+        )
+
+    barrier = pltpu.get_barrier_semaphore()
+
+    @pl.loop(1, devices)
+    def _(k):
+        other = (me + k) % devices
+        pl.semaphore_signal(
+            barrier, inc=1, device_id=place(other // sources, other % sources),
+            device_id_type=pl.DeviceIdType.MESH,
+        )
+
+    hidden_load = pltpu.make_async_copy(hidden_ref, hidden_rows, hidden_sem)
+    hidden_load.start()
+
+    @pl.loop(0, tiles)
+    def _(i):
+        weight_copy(i).start()
+
+    ids = ids_ref[...]
+    labels = iota((tokens, experts), 1)
+    first = (ids[:, 0:1] == labels).astype(f32)
+    second = (ids[:, 1:2] == labels).astype(f32)
+    both = first + second
+    earlier = (iota((tokens, tokens), 1) < iota((tokens, tokens), 0)).astype(f32)
+    before = jnp.dot(earlier, both, preferred_element_type=f32)
+    spread_rows = ((iota((rows, experts), 0) >> 4) == iota((rows, experts), 1)).astype(f32)
+    hit = lax.dot_general(spread_rows, both, CONTRACT_LAST, preferred_element_type=f32)
+    rank = lax.dot_general(spread_rows, before, CONTRACT_LAST, preferred_element_type=f32)
+    slot = (iota((rows, tokens), 0) & (PAD - 1)).astype(f32)
+    table = jnp.where((hit > 0.5) & (jnp.abs(rank - slot) < 0.5), 1.0, 0.0).astype(f32)
+    send_grad[...] = (
+        jnp.dot(table.astype(bf16), grad_ref[...], preferred_element_type=f32)
+        .astype(bf16)
+        .reshape(send_grad.shape)
+    )
+
+    pl.semaphore_wait(barrier, devices - 1)
+
+    input_copies = []
+    for k in range(1, tensor_ranks):
+        to = (tensor + k) % tensor_ranks
+        copy = remote(
+            router_input_ref.at[pl.ds(pl.multiple_of(to * tokens, tokens), tokens)],
+            full_input.at[tensor], input_send.at[k], input_recv.at[tensor],
+            {"tensor": to},
+        )
+        copy.start()
+        input_copies.append(copy)
+    own_input = pltpu.make_async_copy(
+        router_input_ref.at[pl.ds(pl.multiple_of(tensor * tokens, tokens), tokens)],
+        full_input.at[tensor], own_sem.at[0],
+    )
+    own_input.start()
+
+    grad_copies = []
+    for k in range(1, sources):
+        to = (source + k) % sources
+        copy = remote(
+            send_grad.at[to], recv_grad.at[source], grad_send.at[k], grad_recv.at[source],
+            place(group, to),
+        )
+        copy.start()
+        grad_copies.append(copy)
+    own_grad = pltpu.make_async_copy(send_grad.at[source], recv_grad.at[source], own_sem.at[1])
+    own_grad.start()
+
+    hidden_copies = []
+    for k in range(1, groups):
+        to = (group + k) % groups
+        copy = remote(
+            hidden_ref.at[:, pl.ds(pl.multiple_of(to * part, LANES), part)],
+            hidden_all_ref.at[group], hidden_send.at[k], hidden_recv.at[group],
+            {"dp": to},
+        )
+        copy.start()
+        hidden_copies.append(copy)
+
+    own_input.wait()
+    for k in range(1, tensor_ranks):
+        origin = (tensor + k) % tensor_ranks
+        remote(
+            router_input_ref.at[pl.ds(0, tokens)], full_input.at[origin], input_send.at[k],
+            input_recv.at[origin], {"tensor": origin},
+        ).wait_recv()
+    logits = jnp.zeros((tokens, experts), f32)
+    for h in range(tensor_ranks):
+        logits = logits + lax.dot_general(
+            full_input[h], router_weight_ref[:, h * span : (h + 1) * span], CONTRACT_LAST,
+            preferred_element_type=f32,
+        )
+    chosen = jnp.sum(first * logits, axis=1, keepdims=True)
+    rival = jnp.sum(second * logits, axis=1, keepdims=True)
+    first_gate = jax.nn.sigmoid(chosen - rival)
+    second_gate = jax.nn.sigmoid(rival - chosen)
+    gates = first * first_gate + second * second_gate
+    low = gates.astype(bf16).astype(f32)
+    gate_rows = lax.dot_general(
+        spread_rows, low, CONTRACT_LAST, preferred_element_type=f32
+    )
+    slot_gate = jnp.sum(table * gate_rows, axis=1, keepdims=True)
+    send_gate[...] = jnp.broadcast_to(slot_gate, (rows, LANES)).reshape(send_gate.shape)
+    gate_copies = []
+    for k in range(1, sources):
+        to = (source + k) % sources
+        copy = remote(
+            send_gate.at[to], recv_gate.at[source], gate_send.at[k], gate_recv.at[source],
+            place(group, to),
+        )
+        copy.start()
+        gate_copies.append(copy)
+    own_gate = pltpu.make_async_copy(send_gate.at[source], recv_gate.at[source], own_sem.at[2])
+    own_gate.start()
+
+    own_grad.wait()
+    own_gate.wait()
+    for k in range(1, sources):
+        origin = (source + k) % sources
+        remote(
+            send_grad.at[0], recv_grad.at[origin], grad_send.at[k], grad_recv.at[origin],
+            place(group, origin),
+        ).wait_recv()
+        remote(
+            send_gate.at[0], recv_gate.at[origin], gate_send.at[k], gate_recv.at[origin],
+            place(group, origin),
+        ).wait_recv()
+    column = iota((slots, rows), 1)
+    column_slot = column & (PAD - 1)
+    pick = (
+        (iota((slots, rows), 0) == capacity * (column >> 4) + column_slot)
+        & (column_slot < capacity)
+    ).astype(f32)
+    pick_low = pick.astype(bf16)
+    packed_grad = jnp.dot(
+        pick_low, recv_grad[...].reshape(rows, recv_grad.shape[2]), preferred_element_type=f32
+    )
+    packed[...] = packed_grad.astype(bf16)
+    gate_lanes = jnp.dot(
+        pick_low, recv_gate[...].reshape(rows, LANES).astype(bf16), preferred_element_type=f32
+    )
+    gate_column = gate_lanes[:, 0:1]
+    gated_all_ref[pl.ds(group, 1)] = (gate_column * packed_grad).astype(bf16)[None]
+
+    core = group % 2
+    half = group // 2
+    beside = half * 2 + (1 - core)
+    across = (1 - half) * 2 + core
+    diagonal = (1 - half) * 2 + (1 - core)
+    mine = gated_all_ref.at[group]
+    to_across = remote(mine, mine, gated_send.at[0], gated_recv.at[group], {"dp": across})
+    to_across.start()
+    to_beside = remote(mine, mine, gated_send.at[1], gated_recv.at[group], {"dp": beside})
+    to_beside.start()
+
+    hidden_load.wait()
+    own_hidden = pltpu.make_async_copy(
+        hidden_rows.at[:, pl.ds(pl.multiple_of(group * part, LANES), part)],
+        hidden_all_ref.at[group], own_sem.at[3],
+    )
+    own_hidden.start()
+    gate_acc[...] = jnp.zeros_like(gate_acc)
+
+    @pl.loop(0, tiles)
+    def _(i):
+        weight_copy(i).wait()
+        at = pl.ds(pl.multiple_of(i * tile, tile), tile)
+        image = lax.dot_general(
+            packed[...], weights[i], CONTRACT_LAST, preferred_element_type=f32
+        )
+        hidden_grad_ref[:, at] = (gate_column * image).astype(bf16)
+        product = hidden_rows[:, at].astype(f32) * image
+        total = product[:, 0:LANES]
+        for j in range(1, tile // LANES):
+            total = total + product[:, j * LANES : (j + 1) * LANES]
+        gate_acc[...] += total
+
+    partial = jnp.broadcast_to(
+        jnp.sum(gate_acc[...], axis=1, keepdims=True), (slots, LANES)
+    )
+    send_back[...] = lax.dot_general(
+        pick, partial, CONTRACT_FIRST, precision=EXACT, preferred_element_type=f32
+    ).reshape(send_back.shape)
+    back_copies = []
+    for k in range(1, sources):
+        to = (source + k) % sources
+        copy = remote(
+            send_back.at[to], recv_back.at[source], back_send.at[k], back_recv.at[source],
+            place(group, to),
+        )
+        copy.start()
+        back_copies.append(copy)
+    own_back = pltpu.make_async_copy(send_back.at[source], recv_back.at[source], own_sem.at[4])
+    own_back.start()
+
+    theirs = gated_all_ref.at[across]
+    remote(theirs, theirs, gated_send.at[0], gated_recv.at[across], {"dp": across}).wait_recv()
+    relay = remote(theirs, theirs, gated_send.at[2], gated_recv.at[across], {"dp": beside})
+    relay.start()
+
+    own_back.wait()
+    for k in range(1, sources):
+        origin = (source + k) % sources
+        remote(
+            send_back.at[0], recv_back.at[origin], back_send.at[k], back_recv.at[origin],
+            place(group, origin),
+        ).wait_recv()
+    returned = recv_back[...].reshape(rows, LANES)[:, 0:1]
+    gate_grad = lax.dot_general(
+        table * returned, spread_rows, CONTRACT_FIRST, precision=EXACT, preferred_element_type=f32
+    )
+    mixed = jnp.sum(gates * gate_grad, axis=1, keepdims=True)
+    logit_grad = gates * (gate_grad - mixed)
+    chunk = experts // groups
+    block = (span * tensor_ranks) // sources
+    for h in range(tensor_ranks):
+        local = lax.dot_general(
+            logit_grad, full_input[h].astype(f32), CONTRACT_FIRST, precision=EXACT,
+            preferred_element_type=f32,
+        )
+        for b in range(span // block):
+            x = h * (span // block) + b
+            for d in range(groups):
+                send_sum[d * sources + x] = local[
+                    d * chunk : (d + 1) * chunk, b * block : (b + 1) * block
+                ]
+
+    def sum_copy(k, to, slot_at):
+        return remote(
+            send_sum.at[to], recv_sum.at[slot_at], sum_send.at[k], sum_recv.at[slot_at],
+            place(to // sources, to % sources),
+        )
+
+    def whole_copy(k, to, slot_at):
+        return remote(
+            router_grad_ref.at[slot_at], router_grad_ref.at[slot_at], whole_send.at[k],
+            whole_recv.at[slot_at], place(to // sources, to % sources),
+        )
+
+    @pl.loop(1, devices)
+    def _(k):
+        sum_copy(k, (me + k) % devices, me).start()
+
+    recv_sum[pl.ds(me, 1)] = send_sum[pl.ds(me, 1)]
+    input_grad_ref[...] = jnp.dot(
+        logit_grad, router_weight_ref[...].astype(f32), precision=EXACT,
+        preferred_element_type=f32,
+    ).astype(bf16)
+
+    @pl.loop(1, devices)
+    def _(k):
+        origin = (me + k) % devices
+        sum_copy(k, origin, origin).wait_recv()
+
+    router_grad_ref[pl.ds(me, 1)] = jnp.sum(recv_sum[...], axis=0, keepdims=True)
+
+    @pl.loop(1, devices)
+    def _(k):
+        whole_copy(k, (me + k) % devices, me).start()
+
+    @pl.loop(1, devices)
+    def _(k):
+        origin = (me + k) % devices
+        whole_copy(k, origin, origin).wait_recv()
+
+    own_hidden.wait()
+    for k in range(1, groups):
+        origin = (group + k) % groups
+        remote(
+            hidden_ref.at[:, pl.ds(0, part)], hidden_all_ref.at[origin], hidden_send.at[k],
+            hidden_recv.at[origin], {"dp": origin},
+        ).wait_recv()
+    for origin in (beside, diagonal):
+        slab = gated_all_ref.at[origin]
+        remote(
+            slab, slab, gated_send.at[1], gated_recv.at[origin], {"dp": beside}
+        ).wait_recv()
+    for copy in input_copies + grad_copies + hidden_copies + gate_copies + back_copies:
+        copy.wait_send()
+    for copy in (to_across, to_beside, relay):
+        copy.wait_send()
+
+    @pl.loop(1, devices)
+    def _(k):
+        sum_copy(k, (me + k) % devices, me).wait_send()
+        whole_copy(k, (me + k) % devices, me).wait_send()
+
+
+def weight_kernel(hidden_ref, gated_ref, out_ref):
+    out_ref[...] = lax.dot_general(
+        hidden_ref[...], gated_ref[...], CONTRACT_FIRST, preferred_element_type=jnp.float32
+    ).astype(out_ref.dtype)
+
+
+def by_kernels(router_input, router_weight, expert_ids, down_weight, hidden, grad_output):
+    f32, bf16 = jnp.float32, jnp.bfloat16
+    tokens, model = grad_output.shape
+    experts = router_weight.shape[1]
+    groups = lax.axis_size("dp")
+    expert_ranks = lax.axis_size("expert")
+    tensor_ranks = lax.axis_size("tensor")
+    sources = expert_ranks * tensor_ranks
+    devices = groups * sources
+    slots, width = hidden.shape[1:]
+    tile = tile_of(width)
+    span = router_input.shape[1]
+    part = width // groups
+    vmem = pl.BlockSpec(memory_space=pltpu.VMEM)
+    hbm = pl.BlockSpec(memory_space=pl.ANY)
+    dma = pltpu.SemaphoreType.DMA
+    piece = (devices, experts // groups, model // sources)
+    hidden_grad, input_grad, router_parts, hidden_all, gated_all = pl.pallas_call(
+        functools.partial(
+            exchange_kernel, groups, expert_ranks, tensor_ranks, slots // sources, tile
+        ),
+        out_shape=(
+            jax.ShapeDtypeStruct((slots, width), bf16),
+            jax.ShapeDtypeStruct((tokens, model), bf16),
+            jax.ShapeDtypeStruct(piece, f32),
+            jax.ShapeDtypeStruct((groups, slots, part), bf16),
+            jax.ShapeDtypeStruct((groups, slots, model), bf16),
+        ),
+        in_specs=[vmem, vmem, vmem, vmem, hbm, hbm],
+        out_specs=(vmem, vmem, vmem, hbm, vmem),
+        scratch_shapes=[
+            pltpu.VMEM((width // tile, tile, model), bf16),
+            pltpu.VMEM((slots, width), bf16),
+            pltpu.VMEM((tensor_ranks, tokens, span), bf16),
+            pltpu.VMEM((sources, PAD, model), bf16),
+            pltpu.VMEM((sources, PAD, model), bf16),
+            pltpu.VMEM((sources, PAD, LANES), f32),
+            pltpu.VMEM((sources, PAD, LANES), f32),
+            pltpu.VMEM((sources, PAD, LANES), f32),
+            pltpu.VMEM((sources, PAD, LANES), f32),
+            pltpu.VMEM(piece, f32),
+            pltpu.VMEM(piece, f32),
+            pltpu.VMEM((slots, model), bf16),
+            pltpu.VMEM((slots, LANES), f32),
+            dma((width // tile,)),
+            dma,
+            dma((5,)),
+            dma((tensor_ranks,)), dma((tensor_ranks,)),
+            dma((groups,)), dma((groups,)),
+            dma((sources,)), dma((sources,)),
+            dma((sources,)), dma((sources,)),
+            dma((3,)), dma((groups,)),
+            dma((sources,)), dma((sources,)),
+            dma((devices,)), dma((devices,)),
+            dma((devices,)), dma((devices,)),
+        ],
+        compiler_params=pltpu.CompilerParams(
+            collective_id=0, has_side_effects=True, vmem_limit_bytes=VMEM_LIMIT
+        ),
+        name="exchange",
+    )(expert_ids, router_weight.T, grad_output, router_input, down_weight, hidden[0])
+    step = 384 if part % 384 == 0 else LANES
+    weight_grad = pl.pallas_call(
+        weight_kernel,
+        out_shape=jax.ShapeDtypeStruct((part, model), bf16),
+        grid=(part // step,),
+        in_specs=[
+            pl.BlockSpec((groups * slots, step), lambda i: (0, i)),
+            pl.BlockSpec((groups * slots, model), lambda i: (0, 0)),
+        ],
+        out_specs=pl.BlockSpec((step, model), lambda i: (i, 0)),
+        name="weight_grad",
+    )(hidden_all.reshape(groups * slots, part), gated_all.reshape(groups * slots, model))
+    router_grad = (
+        router_parts.reshape(groups, sources, experts // groups, model // sources)
+        .transpose(1, 3, 0, 2)
+        .reshape(model, experts)
+    )
+    return weight_grad, hidden_grad[None], router_grad, input_grad
+
+
+def tile_of(width):
+    for tile in (512, 384, 256):
+        if width % tile == 0:
+            return tile
+    return LANES
+
+
+def kernels_fit(router_input, router_weight, expert_ids, down_weight, hidden, grad_output):
+    groups = lax.axis_size("dp")
+    sources = lax.axis_size("expert") * lax.axis_size("tensor")
+    slots, width = hidden.shape[1:]
+    tokens, model = grad_output.shape
+    experts = router_weight.shape[1]
+    return (
+        groups == 4
+        and sources == experts
+        and experts % groups == 0
+        and slots % 8 == 0
+        and slots // sources <= PAD
+        and tokens % 16 == 0
+        and width % (groups * LANES) == 0
+        and model % (sources * LANES) == 0
+        and 2 * (width * model + 4 * slots * width + 8 * slots * model) < 48 * 1000 * 1000
+    )
+
+
+def per_device(*arrays):
+    return by_kernels(*arrays) if kernels_fit(*arrays) else by_collectives(*arrays)
+
+
+def by_collectives(router_input, router_weight, expert_ids, down_weight, hidden, grad_output):
     token_rows = grad_output.shape[0]
     model_width = grad_output.shape[1]
     expert_count = router_weight.shape[1]

time: 212 us -> 67.3 us (0.32)
  waiting for transfers between devices: 127 us -> 0 us
  Pallas kernels: 0 us -> 61.8 us
  matrix products: 27.5 us -> 0 us
  starting transfers between devices: 20.7 us -> 0 us
  between operations: 15.6 us -> 0.64 us
  local copies, waits for them, and re-layouts: 16.3 us -> 4.54 us
  other arithmetic: 2.78 us -> 0 us
    psum x1 -> x0, waiting for transfers between devices: 89.7 us -> none  [per_device(): router_grad = lax.psum(router_local, ('dp', 'expert', 'tensor'))]
    pallas_call x0 -> x2, Pallas kernels: none -> 61.8 us  [the longest x1 53.7 us: by_kernels(): pl.pallas_call(functools.partial(exchange_kernel, groups, expert_ranks, t...]
    all_to_all x5 -> x0, waiting for transfers between devices: 37.7 us -> none  [the longest x1 13 us: per_device(): lax.all_to_all(hidden_rows, 'dp', split_axis=1, concat_axis=0, tiled=True)]
    dot_general x7 -> x0, matrix products: 27.5 us -> none  [the longest x1 15.6 us: per_device(): lax.dot_general(recv_grad, down_weight, (((1,), (1,)), ((), ())), preferr...]
    all_to_all x5 -> x0, starting transfers between devices: 20.6 us -> none  [the longest x1 5.41 us: per_device(): lax.all_to_all(send_gate, ('expert', 'tensor'), split_axis=0, concat_axis...]
    unnamed x12 -> x8, local copies, waits for them, and re-layouts: 13 us -> 3.7 us
    all_to_all x6 -> x0, local copies, waits for them, and re-layouts: 2.74 us -> none  [the longest x2 1.42 us: per_device(): lax.all_to_all(hidden_rows, 'dp', split_axis=1, concat_axis=0, tiled=True)]
  transfers between devices with their start and end apart: 7 -> 0, of which waited for: 6 -> 0; matrix products, arithmetic and copies ran while one was open for 19% -> 0% of each run, Pallas kernels for 0% -> 0%
where the time goes in v1:
time: 67.3 us; the launch traced here: 67 us
  Pallas kernels  61.8 us (92%)
  local copies, waits for them, and re-layouts  4.54 us (7%)
    pallas_call x1, Pallas kernels, by_kernels(): pl.pallas_call(functools.partial(exchange_kernel, groups, expert_ranks, t...  53.7 us
    pallas_call x1, Pallas kernels, by_kernels(): pl.pallas_call(weight_kernel, out_shape=jax.ShapeDtypeStruct((part, model...  8.06 us
    unnamed x8, local copies, waits for them, and re-layouts  3.7 us

profile of v1, /device:TPU:0, one launch (start us, length us, event | category | flops | bytes accessed | tf_op | source)
XLA Modules:
  0.0 67.0 jit_solution(14769480742413279259)
XLA Ops:
  0.6 1.4 %copy.10.ids_ref = s32[32,2]{1,0:T(8,128)} copy(s32[32,2]{0,1:T(2,128)} %param.8) | data formatting | bytes 512 | tf_op args[2]
  2.0 53.7 %exchange.1 = (bf16[72,7680]{1,0:T(8,128)(2,1)}, bf16[32,2048]{1,0:T(8,128)(2,1)}, f32[32,2,256]{2,1,0:T(2,128)}, bf16[4,72,1920]{2,1,0:T(8,128)(2,1)}, bf16[4,72,2048]{2,1,0:T(8,128)(2,1)}) custom-call(s32[32,2]{1,0:T(8,128)} %copy.10.ids_ref, bf16[8,2048]{1,0:T(8,128)(2,1)} %bitcast.20, bf16[32,2048]{1,0:T(8,128)(2,1)} %grad_ref.1, ...), custom_call_target="tpu_custom_call" | custom-call | tf_op jit(solution)/shard_map/exchange/pallas_call | solution.py:371
  55.7 0.8 %copy.11 = f32[8,256,4,2]{1,0,3,2:T(8,128)S(1)} copy(f32[8,256,4,2]{1,3,0,2:T(2,128)} %bitcast.19) | data formatting | bytes 131072 | tf_op jit(solution)/shard_map/transpose | solution.py:429
  56.6 0.7 copy.12
  57.2 0.0 copy-start
  57.2 8.1 %weight_grad.1 = bf16[1920,2048]{1,0:T(8,128)(2,1)} custom-call(bf16[288,1920]{1,0:T(8,128)(2,1)} %bitcast.16, bf16[288,2048]{1,0:T(8,128)(2,1)} %bitcast.13), custom_call_target="tpu_custom_call" | custom-call | tf_op jit(solution)/shard_map/weight_grad/pallas_call | solution.py:416
  65.3 0.0 copy-done
  65.3 0.0 copy-start.1
  65.3 1.0 %copy.15 = bf16[1,72,7680]{2,1,0:T(8,128)(2,1)} copy(bf16[1,72,7680]{2,1,0:T(8,128)(2,1)S(1)} %bitcast.15) | data formatting | bytes 2211840
  66.3 0.0 copy-done.1
  66.3 0.7 copy.16
Async XLA Ops:
  57.2 8.1 %copy-start = (bf16[72,7680]{1,0:T(8,128)(2,1)S(1)}, bf16[72,7680]{1,0:T(8,128)(2,1)}, u32[]{:S(2)}) copy-start(bf16[72,7680]{1,0:T(8,128)(2,1)} %get-tuple-element.11) | copy-start | bytes 3317764
  65.3 1.0 %copy-start.1 = (bf16[32,2048]{1,0:T(8,128)(2,1)S(1)}, bf16[32,2048]{1,0:T(8,128)(2,1)}, u32[]{:S(2)}) copy-start(bf16[32,2048]{1,0:T(8,128)(2,1)} %get-tuple-element.21) | copy-start | bytes 393220

commit v2 on v1

--- a/solution.py
+++ b/solution.py
@@ -9,6 +9,7 @@
 
 
 PAD = 16
+PIECES = 4
 LANES = 128
 VMEM_LIMIT = 64 * 1000 * 1000
 EXACT = lax.Precision.HIGHEST
@@ -23,10 +24,10 @@
 def exchange_kernel(
     groups, expert_ranks, tensor_ranks, capacity, tile,
     ids_ref, router_weight_ref, grad_ref, router_input_ref, down_ref, hidden_ref,
-    hidden_grad_ref, input_grad_ref, router_grad_ref, hidden_all_ref, gated_all_ref,
+    hidden_grad_ref, input_grad_ref, router_grad_ref, hidden_all_ref, gated_out_ref,
     weights, hidden_rows, full_input, send_grad, recv_grad, send_gate, recv_gate,
-    send_back, recv_back, send_sum, recv_sum, packed, gate_acc,
-    weight_sem, hidden_sem, own_sem,
+    send_back, recv_back, send_sum, recv_sum, packed, gate_acc, gated_all_ref, hidden_out, image_acc,
+    weight_sem, hidden_sem, own_sem, piece_sem, out_sem, gated_out,
     input_send, input_recv, hidden_send, hidden_recv, grad_send, grad_recv,
     gate_send, gate_recv, gated_send, gated_recv, back_send, back_recv,
     sum_send, sum_recv, whole_send, whole_recv,
@@ -77,10 +78,14 @@
     def _(i):
         weight_copy(i).start()
 
-    ids = ids_ref[...]
-    labels = iota((tokens, experts), 1)
-    first = (ids[:, 0:1] == labels).astype(f32)
-    second = (ids[:, 1:2] == labels).astype(f32)
+    labels = iota((experts, tokens), 0)
+    same = (iota((tokens, tokens), 0) == iota((tokens, tokens), 1)).astype(f32)
+    first = lax.dot_general(
+        same, (ids_ref[0:1, :] == labels).astype(f32), CONTRACT_LAST, preferred_element_type=f32
+    )
+    second = lax.dot_general(
+        same, (ids_ref[1:2, :] == labels).astype(f32), CONTRACT_LAST, preferred_element_type=f32
+    )
     both = first + second
     earlier = (iota((tokens, tokens), 1) < iota((tokens, tokens), 0)).astype(f32)
     before = jnp.dot(earlier, both, preferred_element_type=f32)
@@ -89,14 +94,37 @@
     rank = lax.dot_general(spread_rows, before, CONTRACT_LAST, preferred_element_type=f32)
     slot = (iota((rows, tokens), 0) & (PAD - 1)).astype(f32)
     table = jnp.where((hit > 0.5) & (jnp.abs(rank - slot) < 0.5), 1.0, 0.0).astype(f32)
-    send_grad[...] = (
-        jnp.dot(table.astype(bf16), grad_ref[...], preferred_element_type=f32)
-        .astype(bf16)
-        .reshape(send_grad.shape)
-    )
+    wide = grad_ref.shape[1] // PIECES
+    for p in range(PIECES):
+        send_grad[p] = (
+            jnp.dot(
+                table.astype(bf16), grad_ref[:, p * wide : (p + 1) * wide],
+                preferred_element_type=f32,
+            )
+            .astype(bf16)
+            .reshape(send_grad.shape[1:])
+        )
 
     pl.semaphore_wait(barrier, devices - 1)
 
+    grad_copies = []
+
+    def dispatch(p):
+        for k in range(1, sources):
+            to = (source + k) % sources
+            copy = remote(
+                send_grad.at[p, to], recv_grad.at[p, source], grad_send.at[p * sources + k],
+                grad_recv.at[p * sources + source], place(group, to),
+            )
+            copy.start()
+            grad_copies.append(copy)
+        own = pltpu.make_async_copy(
+            send_grad.at[p, source], recv_grad.at[p, source], piece_sem.at[p]
+        )
+        own.start()
+        return own
+
+    own_grads = [dispatch(0)]
     input_copies = []
     for k in range(1, tensor_ranks):
         to = (tensor + k) % tensor_ranks
@@ -113,17 +141,8 @@
     )
     own_input.start()
 
-    grad_copies = []
-    for k in range(1, sources):
-        to = (source + k) % sources
-        copy = remote(
-            send_grad.at[to], recv_grad.at[source], grad_send.at[k], grad_recv.at[source],
-            place(group, to),
-        )
-        copy.start()
-        grad_copies.append(copy)
-    own_grad = pltpu.make_async_copy(send_grad.at[source], recv_grad.at[source], own_sem.at[1])
-    own_grad.start()
+    for p in range(1, PIECES):
+        own_grads.append(dispatch(p))
 
     hidden_copies = []
     for k in range(1, groups):
@@ -135,6 +154,39 @@
         )
         copy.start()
         hidden_copies.append(copy)
+
+    column = iota((slots, rows), 1)
+    column_slot = column & (PAD - 1)
+    pick = (
+        (iota((slots, rows), 0) == capacity * (column >> 4) + column_slot)
+        & (column_slot < capacity)
+    ).astype(f32)
+    pick_low = pick.astype(bf16)
+
+    def receive(p):
+        own_grads[p].wait()
+        for k in range(1, sources):
+            origin = (source + k) % sources
+            remote(
+                send_grad.at[p, 0], recv_grad.at[p, origin], grad_send.at[p * sources + k],
+                grad_recv.at[p * sources + origin], place(group, origin),
+            ).wait_recv()
+        packed[p] = jnp.dot(
+            pick_low, recv_grad[p].reshape(rows, wide), preferred_element_type=f32
+        ).astype(bf16)
+
+    def image_piece(p, i):
+        return lax.dot_general(
+            packed[p], weights[i, :, p * wide : (p + 1) * wide], CONTRACT_LAST,
+            preferred_element_type=f32,
+        )
+
+    receive(0)
+
+    @pl.loop(0, tiles)
+    def _(i):
+        weight_copy(i).wait()
+        image_acc[i] = image_piece(0, i)
 
     own_input.wait()
     for k in range(1, tensor_ranks):
@@ -172,34 +224,29 @@
     own_gate = pltpu.make_async_copy(send_gate.at[source], recv_gate.at[source], own_sem.at[2])
     own_gate.start()
 
-    own_grad.wait()
+    for p in range(1, PIECES - 1):
+        receive(p)
+
+        @pl.loop(0, tiles)
+        def _(i):
+            image_acc[i] += image_piece(p, i)
+
+    receive(PIECES - 1)
     own_gate.wait()
     for k in range(1, sources):
         origin = (source + k) % sources
         remote(
-            send_grad.at[0], recv_grad.at[origin], grad_send.at[k], grad_recv.at[origin],
-            place(group, origin),
-        ).wait_recv()
-        remote(
             send_gate.at[0], recv_gate.at[origin], gate_send.at[k], gate_recv.at[origin],
             place(group, origin),
         ).wait_recv()
-    column = iota((slots, rows), 1)
-    column_slot = column & (PAD - 1)
-    pick = (
-        (iota((slots, rows), 0) == capacity * (column >> 4) + column_slot)
-        & (column_slot < capacity)
-    ).astype(f32)
-    pick_low = pick.astype(bf16)
-    packed_grad = jnp.dot(
-        pick_low, recv_grad[...].reshape(rows, recv_grad.shape[2]), preferred_element_type=f32
-    )
-    packed[...] = packed_grad.astype(bf16)
     gate_lanes = jnp.dot(
         pick_low, recv_gate[...].reshape(rows, LANES).astype(bf16), preferred_element_type=f32
     )
     gate_column = gate_lanes[:, 0:1]
-    gated_all_ref[pl.ds(group, 1)] = (gate_column * packed_grad).astype(bf16)[None]
+    for p in range(PIECES):
+        gated_all_ref[pl.ds(group, 1), :, p * wide : (p + 1) * wide] = (
+            gate_column * packed[p].astype(f32)
+        ).astype(bf16)[None]
 
     core = group % 2
     half = group // 2
@@ -212,6 +259,10 @@
     to_beside = remote(mine, mine, gated_send.at[1], gated_recv.at[group], {"dp": beside})
     to_beside.start()
 
+    def gated_copy(d):
+        return pltpu.make_async_copy(gated_all_ref.at[d], gated_out_ref.at[d], gated_out.at[d])
+
+    gated_copy(group).start()
     hidden_load.wait()
     own_hidden = pltpu.make_async_copy(
         hidden_rows.at[:, pl.ds(pl.multiple_of(group * part, LANES), part)],
@@ -222,18 +273,17 @@
 
     @pl.loop(0, tiles)
     def _(i):
-        weight_copy(i).wait()
         at = pl.ds(pl.multiple_of(i * tile, tile), tile)
-        image = lax.dot_general(
-            packed[...], weights[i], CONTRACT_LAST, preferred_element_type=f32
-        )
-        hidden_grad_ref[:, at] = (gate_column * image).astype(bf16)
+        image = image_acc[i] + image_piece(PIECES - 1, i)
+        hidden_out[:, at] = (gate_column * image).astype(bf16)
         product = hidden_rows[:, at].astype(f32) * image
         total = product[:, 0:LANES]
         for j in range(1, tile // LANES):
             total = total + product[:, j * LANES : (j + 1) * LANES]
         gate_acc[...] += total
 
+    hidden_store = pltpu.make_async_copy(hidden_out, hidden_grad_ref, out_sem)
+    hidden_store.start()
     partial = jnp.broadcast_to(
         jnp.sum(gate_acc[...], axis=1, keepdims=True), (slots, LANES)
     )
@@ -256,6 +306,7 @@
     remote(theirs, theirs, gated_send.at[0], gated_recv.at[across], {"dp": across}).wait_recv()
     relay = remote(theirs, theirs, gated_send.at[2], gated_recv.at[across], {"dp": beside})
     relay.start()
+    gated_copy(across).start()
 
     own_back.wait()
     for k in range(1, sources):
@@ -334,10 +385,14 @@
         remote(
             slab, slab, gated_send.at[1], gated_recv.at[origin], {"dp": beside}
         ).wait_recv()
+        gated_copy(origin).start()
     for copy in input_copies + grad_copies + hidden_copies + gate_copies + back_copies:
         copy.wait_send()
     for copy in (to_across, to_beside, relay):
         copy.wait_send()
+    for d in (group, beside, across, diagonal):
+        gated_copy(d).wait()
+    hidden_store.wait()
 
     @pl.loop(1, devices)
     def _(k):
@@ -345,7 +400,22 @@
         whole_copy(k, (me + k) % devices, me).wait_send()
 
 
-def weight_kernel(hidden_ref, gated_ref, out_ref):
+def weight_kernel(
+    sources, hidden_ref, gated_ref, hidden_grad_ref, input_grad_ref, router_ref,
+    out_ref, hidden_grad_out, input_grad_out, router_out,
+):
+    hidden_grad_out[...] = hidden_grad_ref[...]
+
+    @pl.when(pl.program_id(0) == 0)
+    def _():
+        input_grad_out[...] = input_grad_ref[...]
+        pieces, chunk, block = router_ref.shape
+        for piece in range(pieces):
+            d, x = piece // sources, piece % sources
+            router_out[d * chunk : (d + 1) * chunk, x * block : (x + 1) * block] = router_ref[
+                piece
+            ]
+
     out_ref[...] = lax.dot_general(
         hidden_ref[...], gated_ref[...], CONTRACT_FIRST, preferred_element_type=jnp.float32
     ).astype(out_ref.dtype)
@@ -380,27 +450,33 @@
             jax.ShapeDtypeStruct((groups, slots, model), bf16),
         ),
         in_specs=[vmem, vmem, vmem, vmem, hbm, hbm],
-        out_specs=(vmem, vmem, vmem, hbm, vmem),
+        out_specs=(hbm, vmem, vmem, hbm, hbm),
         scratch_shapes=[
             pltpu.VMEM((width // tile, tile, model), bf16),
             pltpu.VMEM((slots, width), bf16),
             pltpu.VMEM((tensor_ranks, tokens, span), bf16),
-            pltpu.VMEM((sources, PAD, model), bf16),
-            pltpu.VMEM((sources, PAD, model), bf16),
+            pltpu.VMEM((PIECES, sources, PAD, model // PIECES), bf16),
+            pltpu.VMEM((PIECES, sources, PAD, model // PIECES), bf16),
             pltpu.VMEM((sources, PAD, LANES), f32),
             pltpu.VMEM((sources, PAD, LANES), f32),
             pltpu.VMEM((sources, PAD, LANES), f32),
             pltpu.VMEM((sources, PAD, LANES), f32),
             pltpu.VMEM(piece, f32),
             pltpu.VMEM(piece, f32),
-            pltpu.VMEM((slots, model), bf16),
+            pltpu.VMEM((PIECES, slots, model // PIECES), bf16),
             pltpu.VMEM((slots, LANES), f32),
+            pltpu.VMEM((groups, slots, model), bf16),
+            pltpu.VMEM((slots, width), bf16),
+            pltpu.VMEM((width // tile, slots, tile), f32),
             dma((width // tile,)),
             dma,
             dma((5,)),
+            dma((PIECES,)),
+            dma,
+            dma((groups,)),
             dma((tensor_ranks,)), dma((tensor_ranks,)),
             dma((groups,)), dma((groups,)),
-            dma((sources,)), dma((sources,)),
+            dma((PIECES * sources,)), dma((PIECES * sources,)),
             dma((sources,)), dma((sources,)),
             dma((3,)), dma((groups,)),
             dma((sources,)), dma((sources,)),
@@ -411,25 +487,39 @@
             collective_id=0, has_side_effects=True, vmem_limit_bytes=VMEM_LIMIT
         ),
         name="exchange",
-    )(expert_ids, router_weight.T, grad_output, router_input, down_weight, hidden[0])
+    )(expert_ids.T, router_weight.T, grad_output, router_input, down_weight, hidden[0])
     step = 384 if part % 384 == 0 else LANES
-    weight_grad = pl.pallas_call(
-        weight_kernel,
-        out_shape=jax.ShapeDtypeStruct((part, model), bf16),
-        grid=(part // step,),
+    steps = part // step
+    slab = width // steps
+    weight_grad, hidden_grad, input_grad, router_grad = pl.pallas_call(
+        functools.partial(weight_kernel, sources),
+        out_shape=(
+            jax.ShapeDtypeStruct((part, model), bf16),
+            jax.ShapeDtypeStruct((slots, width), bf16),
+            jax.ShapeDtypeStruct((tokens, model), bf16),
+            jax.ShapeDtypeStruct((experts, model), f32),
+        ),
+        grid=(steps,),
         in_specs=[
             pl.BlockSpec((groups * slots, step), lambda i: (0, i)),
             pl.BlockSpec((groups * slots, model), lambda i: (0, 0)),
+            pl.BlockSpec((slots, slab), lambda i: (0, i)),
+            pl.BlockSpec((tokens, model), lambda i: (0, 0)),
+            pl.BlockSpec(piece, lambda i: (0, 0, 0)),
         ],
-        out_specs=pl.BlockSpec((step, model), lambda i: (i, 0)),
+        out_specs=(
+            pl.BlockSpec((step, model), lambda i: (i, 0)),
+            pl.BlockSpec((slots, slab), lambda i: (0, i)),
+            pl.BlockSpec((tokens, model), lambda i: (0, 0)),
+            pl.BlockSpec((experts, model), lambda i: (0, 0)),
+        ),
         name="weight_grad",
-    )(hidden_all.reshape(groups * slots, part), gated_all.reshape(groups * slots, model))
-    router_grad = (
-        router_parts.reshape(groups, sources, experts // groups, model // sources)
-        .transpose(1, 3, 0, 2)
-        .reshape(model, experts)
-    )
-    return weight_grad, hidden_grad[None], router_grad, input_grad
+    )(
+        hidden_all.reshape(groups * slots, part),
+        gated_all.reshape(groups * slots, model),
+        hidden_grad, input_grad, router_parts,
+    )
+    return weight_grad, hidden_grad[None], router_grad.T, input_grad
 
 
 def tile_of(width):
@@ -454,6 +544,7 @@
         and tokens % 16 == 0
         and width % (groups * LANES) == 0
         and model % (sources * LANES) == 0
+        and model % (PIECES * LANES) == 0
         and 2 * (width * model + 4 * slots * width + 8 * slots * model) < 48 * 1000 * 1000
     )
 

time: 67.3 us -> 62.9 us (0.935)
  local copies, waits for them, and re-layouts: 4.54 us -> 0 us
    unnamed x8 -> x0, local copies, waits for them, and re-layouts: 3.7 us -> none
    pallas_call x1, Pallas kernels: 8.06 us -> 9 us  [by_kernels(): pl.pallas_call(functools.partial(weight_kernel, sources), out_shape=(jax....]
    transpose x1 -> x0, local copies, waits for them, and re-layouts: 0.85 us -> none  [by_kernels(): router_grad = router_parts.reshape(groups, sources, experts // groups, mo...]
    pallas_call x1, Pallas kernels: 53.7 us -> 53 us  [by_kernels(): pl.pallas_call(functools.partial(exchange_kernel, groups, expert_ranks, t...]
where the time goes in v2:
time: 62.9 us; the launch traced here: 62.7 us
  Pallas kernels  62 us (99%)
  between operations  0.64 us (1%)
    pallas_call x1, Pallas kernels, by_kernels(): pl.pallas_call(functools.partial(exchange_kernel, groups, expert_ranks, t...  53 us
    pallas_call x1, Pallas kernels, by_kernels(): pl.pallas_call(functools.partial(weight_kernel, sources), out_shape=(jax....  9 us

profile of v2, /device:TPU:0, one launch (start us, length us, event | category | flops | bytes accessed | tf_op | source)
XLA Modules:
  0.0 62.7 jit_solution(12733066151354954859)
XLA Ops:
  0.6 53.0 %exchange.1 = (bf16[72,7680]{1,0:T(8,128)(2,1)}, bf16[32,2048]{1,0:T(8,128)(2,1)}, f32[32,2,256]{2,1,0:T(2,128)}, bf16[4,72,1920]{2,1,0:T(8,128)(2,1)}, bf16[4,72,2048]{2,1,0:T(8,128)(2,1)}) custom-call(s32[2,32]{1,0:T(2,128)} %bitcast.11, bf16[8,2048]{1,0:T(8,128)(2,1)} %bitcast.10, bf16[32,2048]{1,0:T(8,128)(2,1)} %grad_ref.1, ...), custom_call_target="tpu_custom_call" | custom-call | tf_op jit(solution)/shard_map/exchange/pallas_call | solution.py:441
  53.7 9.0 %weight_grad.1 = (bf16[1920,2048]{1,0:T(8,128)(2,1)}, bf16[72,7680]{1,0:T(8,128)(2,1)}, bf16[32,2048]{1,0:T(8,128)(2,1)}, f32[8,2048]{1,0:T(8,128)}) custom-call(bf16[288,1920]{1,0:T(8,128)(2,1)} %bitcast.9, bf16[288,2048]{1,0:T(8,128)(2,1)} %bitcast.7, bf16[72,7680]{1,0:T(8,128)(2,1)} %get-tuple-element.15.hidden_grad_ref, ...), custom_call_target="tpu_custom_call" | custom-call | tf_op jit(solution)/shard_map/weight_grad/pallas_call | solution.py:494
